TPU v7x, 1024 devices: a whole 4x4x32 slice. The times are simulated.
1024 devices in a mesh: lat: 32 (over x, y, core), lon: 32 (over z).
Axes of the slice: x: 4, y: 4, z: 32, core: 2. Of those that a mesh axis runs over, the one named last changes fastest.
Arguments:
- prediction_deviation: bfloat16 [16, 1024, 1024, 80], P(None, 'lat', 'lon'), may hold values from -6 to 6
- humid_energy_misfit: float32 [16, 1024, 1024], P(None, 'lat', 'lon'), may hold values from -0.6 to 0.6
- sensor_space_deviation: bfloat16 [32, 32, 80, 1024], P('lat', 'lon'), may hold values from -6 to 6
- scaled_departure: float32 [32, 32, 1024], P('lat', 'lon'), may hold values from -6 to 6
- datum_location: int32 [32, 32, 2, 1024], P('lat', 'lon'), may hold values from 0 to 31, as said below
- taper_category: int32 [32, 32, 1024], P('lat', 'lon'), may hold values from 0 to 3
- datum_patch_codes: int32 [32, 32, 4, 1024], P('lat', 'lon'), may hold values from -1 to 8, as said below
- active_datum_tally: int32 [32, 32], P('lat', 'lon'), may hold values from 128 to 1024, as said below
Outputs:
- impact: float32 [32, 32, 1024], P('lat', 'lon')
Inputs may be any that keep to these rules, and one draw needn't show every extreme that they name: `datum_location`: row and column of the observation's cell, each from 0 to 31. `datum_patch_codes`: codes are 3 (dr + 1) + (ds + 1) for a tile offset (dr, ds) from the owner, or -1 for an empty entry. Entry 0 is always 4, the owner; the named codes of a slot are distinct and never name a tile beyond the first or last tile row. At least 128 live slots on every tile, and 1024 on some tile in every draw; slots from active_datum_tally on carry no observation.
All inputs are finite; a program needn't handle non-finite values.
Results may differ from a plain program's by a relative error of at most 0.0055.
Values may be sent and summed in bfloat16 or wider, within the bound.
No kernel may reach another device: no remote copies, remote signals or barrier semaphores. Data moves between devices by JAX's collectives and lax.ppermute only.
A program may use at most 32 MiB of HBM per device.

v0:
```python
import jax
import jax.numpy as jnp
from jax import lax
from jax.sharding import PartitionSpec as P


def padded(block, sides, width):
    for axis, dim in sides:
        count = lax.axis_size(axis)
        forward = [(i, i + 1) for i in range(count - 1)]
        forward.append((count - 1, 0))
        backward = [(target, source) for source, target in forward]
        low = lax.ppermute(
            lax.slice_in_dim(block, block.shape[dim] - width, None, axis=dim), axis, forward
        )
        high = lax.ppermute(lax.slice_in_dim(block, 0, width, axis=dim), axis, backward)
        block = jnp.concatenate([low, block, high], axis=dim)
    return block


def taper_weights(obs_row, obs_col, obs_class, cell_rows, cell_cols, allowed, patch_span_points):
    radius = patch_span_points * (1.0 + obs_class) * 0.125
    radius_sq = (radius * radius)[:, None]
    distance = (cell_rows[None, :] - obs_row[:, None]) ** 2 + (
        cell_cols[None, :] - obs_col[:, None]
    ) ** 2
    fraction = 1.0 - distance / radius_sq
    return jnp.where(allowed & (distance < radius_sq), fraction * fraction, 0.0).astype(
        jnp.bfloat16
    )


def tile_offset(shifted, patch_span_points):
    return (shifted >= patch_span_points).astype(jnp.int32) - (shifted < 0).astype(jnp.int32)


def on_device(
    prediction_deviation,
    humid_energy_misfit,
    sensor_space_deviation,
    scaled_departure,
    datum_location,
    taper_category,
    datum_patch_codes,
    active_datum_tally,
):
    patch_span_points = prediction_deviation.shape[1]
    perturbed_runs = prediction_deviation.shape[3]
    slot_count = sensor_space_deviation.shape[3]
    projected = jnp.sum(
        prediction_deviation.astype(jnp.float32) * humid_energy_misfit[..., None], axis=0
    ).astype(jnp.bfloat16)
    margin = patch_span_points // 2
    window_width = 2 * patch_span_points
    window = padded(projected, (("lat", 0), ("lon", 1)), margin)
    offsets = jnp.arange(window_width, dtype=jnp.int32) - margin
    cover_codes = datum_patch_codes[0, 0]
    position = datum_location[0, 0].astype(jnp.float32)
    taper_size = taper_category[0, 0].astype(jnp.float32)
    block_rows = patch_span_points // 2
    projection = jnp.zeros((slot_count, perturbed_runs), jnp.float32)
    for quarter in range(4):
        row_offsets = offsets[quarter * block_rows : (quarter + 1) * block_rows]
        rel_rows = jnp.repeat(row_offsets, window_width)
        rel_cols = jnp.tile(offsets, block_rows)
        tile_code = (
            3 * (tile_offset(rel_rows, patch_span_points) + 1)
            + tile_offset(rel_cols, patch_span_points)
            + 1
        )
        allowed = jnp.any(cover_codes[:, :, None] == tile_code[None, None, :], axis=0)
        weights = taper_weights(
            position[0],
            position[1],
            taper_size,
            rel_rows.astype(jnp.float32),
            rel_cols.astype(jnp.float32),
            allowed,
            patch_span_points,
        )
        window_block = window[quarter * block_rows : (quarter + 1) * block_rows].reshape(
            -1, perturbed_runs
        )
        projection = projection + jnp.dot(weights, window_block, preferred_element_type=jnp.float32)
    summed = jnp.sum(projection * sensor_space_deviation[0, 0].T.astype(jnp.float32), axis=1)
    live_slots = (jnp.arange(slot_count, dtype=jnp.int32) < active_datum_tally[0, 0]).astype(
        jnp.float32
    )
    impact = scaled_departure[0, 0] * summed / (perturbed_runs - 1) * live_slots
    return impact[None, None]


def solution(mesh):
    return jax.shard_map(
        on_device,
        mesh=mesh,
        in_specs=(
            P(None, "lat", "lon", None),
            P(None, "lat", "lon"),
            P("lat", "lon", None, None),
            P("lat", "lon", None),
            P("lat", "lon", None, None),
            P("lat", "lon", None),
            P("lat", "lon", None, None),
            P("lat", "lon"),
        ),
        out_specs=P("lat", "lon", None),
        check_vma=False,
    )
```

profile of v0, /device:TPU:31, one launch (start us, length us, event | category | flops | bytes accessed | tf_op | source)
XLA Modules:
  0.0 75.8 jit_solution(12193506902242170839)
XLA Ops:
  0.0 0.0 copy-start.2
  0.0 0.0 copy-start.1
  0.0 4.5 %multiply_reduce_fusion = bf16[32,32,80]{2,1,0:T(8,128)(2,1)S(1)} fusion(bf16[16,32,32,80]{3,2,1,0:T(8,128)(2,1)} %param.8, f32[16,32,32]{2,1,0:T(8,128)} %param.9), kind=kLoop, calls=%fused_computation.4 | loop fusion | flops 3850240 | bytes 2850816 | tf_op jit(solution)/shard_map/reduce_sum | solution.py:50
  4.5 0.7 fusion.42
  5.2 2.6 %collective-permute-start.1 = (bf16[16,32,80]{2,1,0:T(8,128)(2,1)}, bf16[16,32,80]{2,1,0:T(8,128)(2,1)S(1)}, u32[]{:S(2)}, u32[]{:S(2)}) collective-permute-start(bf16[16,32,80]{2,1,0:T(8,128)(2,1)} %get-tuple-element.16), channel_id=1, source_target_pairs={{32,0},{64,32},{96,64},{128,96},{160,128},{192,160},{224,192},{256... | collective-permute-start | bytes 245768 | tf_op jit(solution)/shard_map/ppermute | solution.py:16
  7.8 14.3 %collective-permute-start = (bf16[16,32,80]{2,1,0:T(8,128)(2,1)}, bf16[16,32,80]{2,1,0:T(8,128)(2,1)}, u32[]{:S(2)}, u32[]{:S(2)}) collective-permute-start(bf16[16,32,80]{2,1,0:T(8,128)(2,1)} %get-tuple-element.15), channel_id=1, source_target_pairs={{0,32},{32,64},{64,96},{96,128},{128,160},{160,192},{192,224},{224... | collective-permute-start | bytes 245768 | tf_op jit(solution)/shard_map/ppermute | solution.py:13
  22.1 0.7 slice_convert_fusion
  22.8 0.1 add_add_fusion.3
  22.8 0.7 reshape.241
  23.5 0.7 reshape.237
  24.2 0.7 reshape.239
  24.8 0.7 reshape.235
  25.5 0.1 broadcast_in_dim.49
  25.6 0.7 convert_element_type.240
  26.2 0.0 copy-done.2
  26.2 0.6 fusion.43
  26.8 0.0 copy-done.1
  26.8 13.2 %compare_reduce_fusion = (pred[1024,1024]{1,0:T(8,128)(4,1)S(1)}, pred[1024,1024]{1,0:T(8,128)(4,1)}, pred[1024,1024]{1,0:T(8,128)(4,1)S(1)}, pred[1024,1024]{1,0:T(8,128)(4,1)S(1)}) fusion(s32[1024]{0:T(1024)} %reshape.241, s32[4,1024]{1,0:T(4,128)S(1)} %bitcast.26, s32[1024]{0:T(1024)} %reshape.237, s32[1024]{0:T(1024)} %reshape.239, s32[1024]{0:T(1024)} %reshape.235), kind=kLoop, calls=%fused_computation | loop fusion | flops 29360128 | bytes 4227072 | tf_op jit(solution)/shard_map/reduce_or | solution.py:71
  40.0 0.0 copy-start.4
  40.0 0.1 convert_element_type.232
  40.1 0.8 broadcast_in_dim.46
  40.8 0.7 convert_element_type.229
  41.5 0.6 broadcast_in_dim.51
  42.1 0.7 convert_element_type.245
  42.8 0.7 broadcast_in_dim.53
  43.5 0.7 convert_element_type.250
  44.2 0.0 copy-start
  44.2 0.0 copy-start.8
  44.2 0.0 copy-start.9
  44.9 0.0 collective-permute-done.1
  45.0 0.0 collective-permute-done
  45.0 1.0 %pad_maximum_fusion.1 = bf16[64,32,80]{2,1,0:T(8,128)(2,1)S(1)} fusion(bf16[16,32,80]{2,1,0:T(8,128)(2,1)S(1)} %collective-permute-done.1, bf16[32,32,80]{2,1,0:T(8,128)(2,1)S(1)} %multiply_reduce_fusion, bf16[16,32,80]{2,1,0:T(8,128)(2,1)} %collective-permute-done), kind=kLoop, calls=%fused_computation.32 | loop fusion | flops 327680 | bytes 655360 | tf_op jit(solution)/shard_map/concatenate | solution.py:17
  46.0 10.4 %collective-permute-start.3 = (bf16[64,16,80]{2,1,0:T(8,128)(2,1)S(1)}, bf16[64,16,80]{2,1,0:T(8,128)(2,1)S(1)}, u32[]{:S(2)}, u32[]{:S(2)}) collective-permute-start(bf16[64,16,80]{2,1,0:T(8,128)(2,1)S(1)} %get-tuple-element.14), channel_id=1, source_target_pairs={{1,0},{2,1},{3,2},{4,3},{5,4},{6,5},{7,6},{8,7},{9,8},{10,9},{11,1... | collective-permute-start | bytes 491528 | tf_op jit(solution)/shard_map/ppermute | solution.py:16
  56.5 2.1 %collective-permute-start.2 = (bf16[64,16,80]{2,1,0:T(8,128)(2,1)S(1)}, bf16[64,16,80]{2,1,0:T(8,128)(2,1)S(1)}, u32[]{:S(2)}, u32[]{:S(2)}) collective-permute-start(bf16[64,16,80]{2,1,0:T(8,128)(2,1)S(1)} %get-tuple-element.13), channel_id=1, source_target_pairs={{0,1},{1,2},{2,3},{3,4},{4,5},{5,6},{6,7},{7,8},{8,9},{9,10},{10,1... | collective-permute-start | bytes 491528 | tf_op jit(solution)/shard_map/ppermute | solution.py:13
  58.6 0.7 multiply_multiply_fusion
  59.3 0.5 collective-permute-done.3
  59.8 5.0 %collective-permute-done.2 = bf16[64,16,80]{2,1,0:T(8,128)(2,1)S(1)} collective-permute-done((bf16[64,16,80]{2,1,0:T(8,128)(2,1)S(1)}, bf16[64,16,80]{2,1,0:T(8,128)(2,1)S(1)}, u32[]{:S(2)}, u32[]{:S(2)}) %collective-permute-start.2) | collective-permute-done | bytes 163872 | tf_op jit(solution)/shard_map/ppermute | solution.py:13
  64.8 1.2 %pad_maximum_fusion = bf16[64,64,80]{2,1,0:T(8,128)(2,1)S(1)} fusion(bf16[64,16,80]{2,1,0:T(8,128)(2,1)S(1)} %collective-permute-done.3, bf16[16,32,80]{2,1,0:T(8,128)(2,1)S(1)} %collective-permute-done.1, bf16[32,32,80]{2,1,0:T(8,128)(2,1)S(1)} %multiply_reduce_fusion, bf16[16,32,80]{2,1,0:T(8,128)(2,1)} %collective-permute-done, ...), kind=kLoop, calls=%fused_computation.31 | loop fusion | flops 3276800 | bytes 1310720 | tf_op jit(solution)/shard_map/concatenate | solution.py:17
  66.0 0.1 fusion.40
  66.1 0.0 copy-done.4
  66.1 0.0 copy-done
  66.1 0.0 copy-done.8
  66.1 0.0 copy-done.9
  66.1 0.0 copy-start.7
  66.1 2.2 %fusion.10 = f32[1024,80]{0,1:T(8,128)S(1)} fusion(bf16[1024,80]{1,0:T(8,128)(2,1)S(1)} %bitcast.25, pred[1024,1024]{1,0:T(8,128)(4,1)S(1)} %copy-done, f32[1024]{0:T(1024)S(1)} %copy-done.4, f32[1024]{0:T(1024)S(1)} %bitcast.28, f32[1024]{0:T(1024)S(1)} %bitcast.36, f32[1024]{0:T(1024)S(1)} %convert_element_type.232, f32[1024]{0:T(1024)S(1)} %bitcast.32), kind=kOutput, calls=%fused_computation.23 | convolution fusion | flops 180355072 | bytes 1560576 | tf_op jit(solution)/shard_map/dot_general | solution.py:84
  68.3 0.0 copy-done.7
  68.3 0.0 copy-start.6
  68.3 2.2 %fusion.16 = f32[1024,80]{0,1:T(8,128)S(1)} fusion(f32[1024,80]{0,1:T(8,128)S(1)} %fusion.10, bf16[1024,80]{1,0:T(8,128)(2,1)S(1)} %bitcast.24, pred[1024,1024]{1,0:T(8,128)(4,1)S(1)} %get-tuple-element.8, f32[1024]{0:T(1024)S(1)} %bitcast.29, f32[1024]{0:T(1024)S(1)} %bitcast.37, f32[1024]{0:T(1024)S(1)} %convert_element_type.232, f32[1024]{0:T(1024)S(1)} %bitcast.33, ...), kind=kOutput, calls=%fused_computation.29 | convolution fusion | flops 180436992 | bytes 1888256 | tf_op jit(solution)/shard_map/dot_general | solution.py:84
  70.5 0.0 copy-done.6
  70.5 0.0 copy-start.5
  70.5 0.0 copy-start.10
  70.5 2.2 %fusion.15 = f32[1024,80]{0,1:T(8,128)S(1)} fusion(f32[1024,80]{0,1:T(8,128)S(1)} %fusion.16, bf16[1024,80]{1,0:T(8,128)(2,1)S(1)} %bitcast.23, pred[1024,1024]{1,0:T(8,128)(4,1)S(1)} %get-tuple-element.7, f32[1024]{0:T(1024)S(1)} %copy-done.6, f32[1024]{0:T(1024)S(1)} %bitcast.30, f32[1024]{0:T(1024)S(1)} %bitcast.38, f32[1024]{0:T(1024)S(1)} %convert_element_type.232, ...), kind=kOutput, calls=%fused_computation.28 | convolution fusion | flops 180436992 | bytes 1888256 | tf_op jit(solution)/shard_map/dot_general | solution.py:84
  72.7 0.0 copy-done.5
  72.7 0.0 copy-done.10
  72.7 0.0 copy-start.3
  72.8 2.5 %fusion.17 = f32[1024]{0:T(1024)S(1)} fusion(f32[1024,80]{0,1:T(8,128)S(1)} %fusion.15, bf16[1024,80]{1,0:T(8,128)(2,1)S(1)} %bitcast.22, pred[1024,1024]{1,0:T(8,128)(4,1)S(1)} %get-tuple-element.5, f32[1024]{0:T(1024)S(1)} %copy-done.5, f32[1024]{0:T(1024)S(1)} %bitcast.31, f32[1024]{0:T(1024)S(1)} %bitcast.39, f32[1024]{0:T(1024)S(1)} %convert_element_type.232, ...), kind=kOutput, calls=%fused_computation.30 | convolution fusion | flops 180681728 | bytes 1728512 | tf_op jit(solution)/shard_map/dot_general | solution.py:84
  75.2 0.0 copy-done.3
  75.2 0.6 compare_select_fusion
  (6 shorter events, 0.1 us)
Async XLA Ops:
  0.0 26.2 %copy-start.2 = (s32[1,1,2,1024]{3,2,1,0:T(2,128)S(1)}, s32[1,1,2,1024]{3,2,1,0:T(2,128)}, u32[]{:S(2)}) copy-start(s32[1,1,2,1024]{3,2,1,0:T(2,128)} %param.12) | copy-start | bytes 24580
  0.0 26.8 %copy-start.1 = (s32[1,1,4,1024]{3,2,1,0:T(4,128)S(1)}, s32[1,1,4,1024]{3,2,1,0:T(4,128)}, u32[]{:S(2)}) copy-start(s32[1,1,4,1024]{3,2,1,0:T(4,128)} %param.14) | copy-start | bytes 49156
  5.2 39.8 %collective-permute-start.1 = (bf16[16,32,80]{2,1,0:T(8,128)(2,1)}, bf16[16,32,80]{2,1,0:T(8,128)(2,1)S(1)}, u32[]{:S(2)}, u32[]{:S(2)}) collective-permute-start(bf16[16,32,80]{2,1,0:T(8,128)(2,1)} %get-tuple-element.16), channel_id=1, source_target_pairs={{32,0},{64,32},{96,64},{128,96},{160,128},{192,160},{224,192},{256... | collective-permute-start | bytes 245768 | tf_op jit(solution)/shard_map/ppermute | solution.py:16
  7.8 37.2 %collective-permute-start = (bf16[16,32,80]{2,1,0:T(8,128)(2,1)}, bf16[16,32,80]{2,1,0:T(8,128)(2,1)}, u32[]{:S(2)}, u32[]{:S(2)}) collective-permute-start(bf16[16,32,80]{2,1,0:T(8,128)(2,1)} %get-tuple-element.15), channel_id=1, source_target_pairs={{0,32},{32,64},{64,96},{96,128},{128,160},{160,192},{192,224},{224... | collective-permute-start | bytes 245768 | tf_op jit(solution)/shard_map/ppermute | solution.py:13
  40.0 26.1 %copy-start.4 = (f32[1024]{0:T(1024)S(1)}, f32[1024]{0:T(1024)}, u32[]{:S(2)}) copy-start(f32[1024]{0:T(1024)} %convert_element_type.240) | copy-start | bytes 12292
  44.2 21.9 %copy-start = (pred[1024,1024]{1,0:T(8,128)(4,1)S(1)}, pred[1024,1024]{1,0:T(8,128)(4,1)}, u32[]{:S(2)}) copy-start(pred[1024,1024]{1,0:T(8,128)(4,1)} %get-tuple-element.6) | copy-start | bytes 3145732
  44.2 21.9 %copy-start.8 = (f32[1,1,1,1024]{3,2,1,0:T(1,128)S(1)}, f32[1,1,1,1024]{3,2,1,0:T(1,128)}, u32[]{:S(2)}) copy-start(f32[1,1,1,1024]{3,2,1,0:T(1,128)} %get-tuple-element.17) | copy-start | bytes 12292
  44.2 21.9 %copy-start.9 = (f32[1,1,1,1024]{3,2,1,0:T(1,128)S(1)}, f32[1,1,1,1024]{3,2,1,0:T(1,128)}, u32[]{:S(2)}) copy-start(f32[1,1,1,1024]{3,2,1,0:T(1,128)} %get-tuple-element.18) | copy-start | bytes 12292
  46.0 13.7 %collective-permute-start.3 = (bf16[64,16,80]{2,1,0:T(8,128)(2,1)S(1)}, bf16[64,16,80]{2,1,0:T(8,128)(2,1)S(1)}, u32[]{:S(2)}, u32[]{:S(2)}) collective-permute-start(bf16[64,16,80]{2,1,0:T(8,128)(2,1)S(1)} %get-tuple-element.14), channel_id=1, source_target_pairs={{1,0},{2,1},{3,2},{4,3},{5,4},{6,5},{7,6},{8,7},{9,8},{10,9},{11,1... | collective-permute-start | bytes 491528 | tf_op jit(solution)/shard_map/ppermute | solution.py:16
  56.5 8.3 %collective-permute-start.2 = (bf16[64,16,80]{2,1,0:T(8,128)(2,1)S(1)}, bf16[64,16,80]{2,1,0:T(8,128)(2,1)S(1)}, u32[]{:S(2)}, u32[]{:S(2)}) collective-permute-start(bf16[64,16,80]{2,1,0:T(8,128)(2,1)S(1)} %get-tuple-element.13), channel_id=1, source_target_pairs={{0,1},{1,2},{2,3},{3,4},{4,5},{5,6},{6,7},{7,8},{8,9},{9,10},{10,1... | collective-permute-start | bytes 491528 | tf_op jit(solution)/shard_map/ppermute | solution.py:13
  66.1 2.2 %copy-start.7 = (f32[1024]{0:T(1024)S(1)}, f32[1024]{0:T(1024)}, u32[]{:S(2)}) copy-start(f32[1024]{0:T(1024)} %convert_element_type.229) | copy-start | bytes 12292
  68.3 2.2 %copy-start.6 = (f32[1024]{0:T(1024)S(1)}, f32[1024]{0:T(1024)}, u32[]{:S(2)}) copy-start(f32[1024]{0:T(1024)} %convert_element_type.245) | copy-start | bytes 12292
  70.5 2.2 %copy-start.5 = (f32[1024]{0:T(1024)S(1)}, f32[1024]{0:T(1024)}, u32[]{:S(2)}) copy-start(f32[1024]{0:T(1024)} %convert_element_type.250) | copy-start | bytes 12292
  70.5 2.2 %copy-start.10 = (bf16[1,1,80,1024]{3,2,1,0:T(8,128)(2,1)S(1)}, bf16[1,1,80,1024]{3,2,1,0:T(8,128)(2,1)}, u32[]{:S(2)}) copy-start(bf16[1,1,80,1024]{3,2,1,0:T(8,128)(2,1)} %param.10) | copy-start | bytes 491524
  72.7 2.5 %copy-start.3 = (f32[1,1,1024]{2,1,0:T(1,128)S(1)}, f32[1,1,1024]{2,1,0:T(1,128)}, u32[]{:S(2)}) copy-start(f32[1,1,1024]{2,1,0:T(1,128)} %param.11) | copy-start | bytes 12292
where the time goes:
time: 76.3 us; the launch traced here: 75.8 us
  starting transfers between devices  29.4 us (39%)
  other arithmetic  21.9 us (29%)
  local copies, waits for them, and re-layouts  9.05 us (12%)
  matrix products  9.01 us (12%)
  waiting for transfers between devices  5.53 us (7%)
  between operations  0.98 us (1%)
    ppermute x2, starting transfers between devices, padded(): lax.ppermute(lax.slice_in_dim(block, block.shape[dim] - width, None, axis...  16.4 us
    reduce_or x1, other arithmetic, on_device(): jnp.any(cover_codes[:, :, None] == tile_code[None, None, :], axis=0)  13.2 us
    ppermute x2, starting transfers between devices, padded(): lax.ppermute(lax.slice_in_dim(block, 0, width, axis=dim), axis, backward)  13 us
    dot_general x4, matrix products, on_device(): jnp.dot(weights, window_block, preferred_element_type=jnp.float32)  9.01 us
    ppermute x2, waiting for transfers between devices, padded(): lax.ppermute(lax.slice_in_dim(block, block.shape[dim] - width, None, axis...  5.03 us
    reduce_sum x1, other arithmetic, on_device(): jnp.sum(prediction_deviation.astype(jnp.float32) * humid_energy_misfit[.....  4.46 us
    convert_element_type x4, local copies, waits for them, and re-layouts, on_device(): rel_rows.astype(jnp.float32)  2.66 us
    add x4, local copies, waits for them, and re-layouts, on_device(): 3 * (tile_offset(rel_rows, patch_span_points) + 1)  2.64 us
  transfers between devices with their start and end apart: 4, of which 2 were waited for; matrix products, arithmetic and copies ran while one was open for 30% of the time, Pallas kernels for 0%

commit v1 on v0

v1 whole, which is shorter than its diff:
```python
import jax
import jax.numpy as jnp
from jax import lax
from jax.experimental import pallas as pl
from jax.experimental.pallas import tpu as pltpu
from jax.sharding import PartitionSpec as P

HALF = 16
CELLS = HALF * HALF
CHUNKS = 4

F32 = jnp.float32
BF16 = jnp.bfloat16


def level_sum_kernel(dev_hbm, misfit_hbm, left_ref, right_ref, dev, misfit_ref, wide, sems):
    levels, rows, cols, runs = dev.shape
    step = rows // CHUNKS
    first = pltpu.make_async_copy(misfit_hbm, misfit_ref, sems.at[CHUNKS])
    first.start()
    copies = []
    for c in range(CHUNKS):
        part = pl.ds(c * step, step)
        copies.append(pltpu.make_async_copy(dev_hbm.at[:, part], dev.at[:, part], sems.at[c]))
        copies[-1].start()
    first.wait()
    for h in range(cols // HALF):
        wide[h] = jnp.concatenate(
            [misfit_ref[l][:, h * HALF : (h + 1) * HALF] for l in range(levels)], axis=1
        )
    depth = levels * HALF
    own = lax.broadcasted_iota(jnp.int32, (HALF, depth), 0)
    lane = lax.broadcasted_iota(jnp.int32, (HALF, depth), 1)
    diagonal = own == lane % HALF
    outs = (left_ref, right_ref)
    for c in range(CHUNKS):
        copies[c].wait()
        for h in range(cols // HALF):
            summed = []
            for y in range(c * step, (c + 1) * step):
                row = jnp.broadcast_to(wide[h, pl.ds(y, 1), :], (HALF, depth))
                row = jnp.where(diagonal, row, 0.0)
                high = row.astype(BF16)
                low = (row - high.astype(F32)).astype(BF16)
                block = dev[:, y, h * HALF : (h + 1) * HALF, :].reshape(depth, runs)
                both = jnp.dot(
                    jnp.concatenate([high, low], axis=0), block, preferred_element_type=F32
                )
                summed.append(both[:HALF] + both[HALF:])
            group = jnp.concatenate(summed, axis=0).T.astype(BF16)
            per = CELLS // (step * HALF)
            width = step * HALF
            outs[h][c // per, :, (c % per) * width : (c % per + 1) * width] = group


def assemble_kernel(low_ref, left_ref, right_ref, high_ref, top_ref, bottom_ref):
    for i, ref in enumerate((low_ref, left_ref, right_ref, high_ref)):
        top_ref[i] = ref[0]
        bottom_ref[i] = ref[1]


def tables(place_ref, class_ref, codes_ref, col_bands, row_bands):
    shape = (HALF, place_ref.shape[1])
    u = jnp.broadcast_to(place_ref[0:1, :], shape).astype(F32).astype(BF16)
    v = place_ref[1:2, :]
    x = lax.broadcasted_iota(jnp.int32, shape, 0)
    side = HALF // 4 * (1 + class_ref[...])
    radius_sq = side * side
    column = {}
    for band in col_bands:
        gap = x + HALF * (band - 1) - v
        column[band] = (gap * gap).astype(F32).astype(BF16)
    reach = {}
    for band_row in row_bands:
        for band in col_bands:
            dr, ds = (band_row + 1) // 2, (band + 1) // 2
            if (dr, ds) in reach:
                continue
            code = 3 * dr + ds
            named = codes_ref[0:1, :] == code
            for e in range(1, 4):
                named = named | (codes_ref[e : e + 1, :] == code)
            kept = jnp.where(named, radius_sq, 0)
            reach[dr, ds] = jnp.broadcast_to(kept, shape).astype(F32).astype(BF16)
    return u, column, reach


def project(window, place_ref, class_ref, codes_ref, blocks):
    col_bands = sorted({b for _, b, _ in blocks})
    row_bands = sorted({a for a, _, _ in blocks})
    u, column, reach = tables(place_ref, class_ref, codes_ref, col_bands, row_bands)
    slots = place_ref.shape[1]
    wide = 256
    parts = []
    for n in range(slots // wide):
        cut = slice(n * wide, (n + 1) * wide)
        total = None
        for row_band in row_bands:
            squares = []
            for y in range(HALF):
                gap = jnp.asarray(y + HALF * (row_band - 1), BF16) - u[:, cut]
                squares.append(gap * gap)
            for a, b, source in blocks:
                if a != row_band:
                    continue
                limit = reach[(a + 1) // 2, (b + 1) // 2][:, cut]
                across = column[b][:, cut]
                pieces = []
                for y in range(HALF):
                    m = jnp.maximum((limit - squares[y]) - across, jnp.asarray(0, BF16))
                    pieces.append(m * m)
                taper = jnp.concatenate(pieces, axis=0)
                term = jnp.dot(window(source), taper, preferred_element_type=F32)
                total = term if total is None else total + term
        parts.append(total)
    return parts


def reduce_kernel(window, blocks, place_ref, class_ref, codes_ref, sensed_ref, out_ref):
    parts = project(window, place_ref, class_ref, codes_ref, blocks)
    for n, part in enumerate(parts):
        wide = part.shape[1]
        cut = slice(n * wide, (n + 1) * wide)
        out_ref[:, cut] = jnp.sum(part * sensed_ref[:, cut].astype(F32), axis=0, keepdims=True)


def inner_kernel(
    tally_hbm,
    left_ref,
    right_ref,
    place_ref,
    class_ref,
    codes_ref,
    sensed_ref,
    scaled_ref,
    out_ref,
    weight_ref,
    tally_ref,
    sem,
):
    copy = pltpu.make_async_copy(tally_hbm, tally_ref, sem)
    copy.start()
    blocks = [(1 + y, 1 + h, (h, y)) for h in range(2) for y in range(2)]
    refs = (left_ref, right_ref)
    reduce_kernel(
        lambda s: refs[s[0]][s[1]], blocks, place_ref, class_ref, codes_ref, sensed_ref, out_ref
    )
    side = (HALF // 4 * (1 + class_ref[...])).astype(F32)
    radius_sq = side * side
    weight = scaled_ref[...] / (radius_sq * radius_sq) / (sensed_ref.shape[0] - 1)
    slot = lax.broadcasted_iota(jnp.int32, weight.shape, 1)
    copy.wait()
    weight_ref[...] = jnp.where(slot < tally_ref[0, 0], weight, 0.0)


def sides_kernel(low_ref, high_ref, place_ref, class_ref, codes_ref, sensed_ref, out_ref):
    blocks = [(1 + y, 3 * h, (h, y)) for h in range(2) for y in range(2)]
    refs = (low_ref, high_ref)
    reduce_kernel(
        lambda s: refs[s[0]][s[1]], blocks, place_ref, class_ref, codes_ref, sensed_ref, out_ref
    )


def outer_kernel(
    above_ref,
    below_ref,
    place_ref,
    class_ref,
    codes_ref,
    sensed_ref,
    inner_ref,
    sides_ref,
    weight_ref,
    out_ref,
):
    blocks = [(3 * h, b, (h, b)) for h in range(2) for b in range(4)]
    refs = (above_ref, below_ref)
    parts = project(lambda s: refs[s[0]][s[1]], place_ref, class_ref, codes_ref, blocks)
    for n, part in enumerate(parts):
        wide = part.shape[1]
        cut = slice(n * wide, (n + 1) * wide)
        summed = jnp.sum(part * sensed_ref[:, cut].astype(F32), axis=0, keepdims=True)
        summed = summed + inner_ref[:, cut] + sides_ref[:, cut]
        out_ref[:, cut] = weight_ref[:, cut] * summed


def on_device(
    prediction_deviation,
    humid_energy_misfit,
    sensor_space_deviation,
    scaled_departure,
    datum_location,
    taper_category,
    datum_patch_codes,
    active_datum_tally,
):
    levels, rows, cols, runs = prediction_deviation.shape
    slots = sensor_space_deviation.shape[3]
    vmem = pl.BlockSpec(memory_space=pltpu.VMEM)
    anywhere = pl.BlockSpec(memory_space=pl.ANY)
    half = pltpu.VMEM((2, runs, CELLS), BF16)
    strip = pltpu.VMEM((4, runs, CELLS), BF16)
    line = pltpu.VMEM((1, slots), F32)

    def near(*arrays):
        return [pltpu.with_memory_space_constraint(a, pltpu.VMEM) for a in arrays]

    left, right = pl.pallas_call(
        level_sum_kernel,
        out_shape=(half, half),
        in_specs=[anywhere, anywhere],
        out_specs=(vmem, vmem),
        scratch_shapes=[
            pltpu.VMEM((levels, rows, cols, runs), BF16),
            pltpu.VMEM((levels, rows, cols), F32),
            pltpu.VMEM((2, rows, levels * HALF), F32),
            pltpu.SemaphoreType.DMA((CHUNKS + 1,)),
        ],
        name="level_sum",
    )(prediction_deviation, humid_energy_misfit)

    def shift(block, axis, by):
        count = lax.axis_size(axis)
        return lax.ppermute(block, axis, [(i, (i + by) % count) for i in range(count)])

    low = shift(right, "lon", 1)
    high = shift(left, "lon", -1)

    place = datum_location[0, 0]
    category = taper_category[0]
    codes = datum_patch_codes[0, 0]
    sensed = sensor_space_deviation[0, 0]

    def cost(blocks):
        flops = 2 * runs * blocks * CELLS * slots
        return pl.CostEstimate(flops=flops, transcendentals=0, bytes_accessed=runs * 4096)

    inner, weight = pl.pallas_call(
        inner_kernel,
        out_shape=(line, line),
        in_specs=[anywhere] + [vmem] * 7,
        out_specs=(vmem, vmem),
        scratch_shapes=[pltpu.SMEM((1, 1), jnp.int32), pltpu.SemaphoreType.DMA],
        cost_estimate=cost(4),
        name="inner",
    )(active_datum_tally, *near(left, right, place, category, codes, sensed, scaled_departure[0]))
    top, bottom = pl.pallas_call(
        assemble_kernel,
        out_shape=(strip, strip),
        in_specs=[vmem] * 4,
        out_specs=(vmem, vmem),
        name="assemble",
    )(*near(low, left, right, high))
    above = shift(bottom, "lat", 1)
    below = shift(top, "lat", -1)
    sides = pl.pallas_call(
        sides_kernel,
        out_shape=line,
        in_specs=[vmem] * 6,
        out_specs=vmem,
        cost_estimate=cost(4),
        name="sides",
    )(*near(low, high, place, category, codes, sensed))
    impact = pl.pallas_call(
        outer_kernel,
        out_shape=jax.ShapeDtypeStruct((1, slots), F32),
        in_specs=[vmem] * 9,
        out_specs=vmem,
        cost_estimate=cost(8),
        name="outer",
    )(*near(above, below, place, category, codes, sensed, inner, sides, weight))
    return impact[None]


def solution(mesh):
    return jax.shard_map(
        on_device,
        mesh=mesh,
        in_specs=(
            P(None, "lat", "lon", None),
            P(None, "lat", "lon"),
            P("lat", "lon", None, None),
            P("lat", "lon", None),
            P("lat", "lon", None, None),
            P("lat", "lon", None),
            P("lat", "lon", None, None),
            P("lat", "lon"),
        ),
        out_specs=P("lat", "lon", None),
        check_vma=False,
    )
```

time: 76.3 us -> 39.6 us (0.52)
  other arithmetic: 21.9 us -> 0 us
  local copies, waits for them, and re-layouts: 9.05 us -> 0.02 us
  matrix products: 9.01 us -> 0 us
  Pallas kernels: 0 us -> 6 us
  starting transfers between devices: 29.4 us -> 25.7 us
  waiting for transfers between devices: 5.53 us -> 6.9 us
    reduce_or x1 -> x0, other arithmetic: 13.2 us -> none  [on_device(): jnp.any(cover_codes[:, :, None] == tile_code[None, None, :], axis=0)]
    dot_general x4 -> x0, matrix products: 9.01 us -> none  [on_device(): jnp.dot(weights, window_block, preferred_element_type=jnp.float32)]
    pallas_call x0 -> x5, Pallas kernels: none -> 6 us  [the longest x1 2.77 us: on_device(): pl.pallas_call(level_sum_kernel, out_shape=(half, half), in_specs=[anywhe...]
    reduce_sum x1 -> x0, other arithmetic: 4.46 us -> none  [on_device(): jnp.sum(prediction_deviation.astype(jnp.float32) * humid_energy_misfit[.....]
    ppermute x4, starting transfers between devices: 29.4 us -> 25.7 us  [shift(): lax.ppermute(block, axis, [(i, (i + by) % count) for i in range(count)])]
    convert_element_type x5 -> x0, local copies, waits for them, and re-layouts: 2.73 us -> none  [the longest x4 2.66 us: on_device(): rel_rows.astype(jnp.float32)]
    add x4 -> x0, local copies, waits for them, and re-layouts: 2.64 us -> none  [on_device(): 3 * (tile_offset(rel_rows, patch_span_points) + 1)]
    concatenate x2 -> x0, other arithmetic: 2.22 us -> none  [padded(): block = jnp.concatenate([low, block, high], axis=dim)]
  transfers between devices with their start and end apart: 4 -> 4, of which waited for: 2 -> 3; matrix products, arithmetic and copies ran while one was open for 30% -> 0% of each run, Pallas kernels for 0% -> 4%
where the time goes in v1:
time: 39.6 us; the launch traced here: 39.4 us
  starting transfers between devices  25.7 us (65%)
  waiting for transfers between devices  6.9 us (17%)
  Pallas kernels  6 us (15%)
  between operations  0.78 us (2%)
    ppermute x4, starting transfers between devices, shift(): lax.ppermute(block, axis, [(i, (i + by) % count) for i in range(count)])  25.7 us
    ppermute x4, waiting for transfers between devices, shift(): lax.ppermute(block, axis, [(i, (i + by) % count) for i in range(count)])  6.9 us
    pallas_call x1, Pallas kernels, on_device(): pl.pallas_call(level_sum_kernel, out_shape=(half, half), in_specs=[anywhe...  2.77 us
    pallas_call x1, Pallas kernels, on_device(): pl.pallas_call(outer_kernel, out_shape=jax.ShapeDtypeStruct((1, slots), F...  1.6 us
    pallas_call x1, Pallas kernels, on_device(): pl.pallas_call(inner_kernel, out_shape=(line, line), in_specs=[anywhere]...  0.99 us
  transfers between devices with their start and end apart: 4, of which 3 were waited for; matrix products, arithmetic and copies ran while one was open for 0% of the time, Pallas kernels for 4%

profile of v1, /device:TPU:31, one launch (start us, length us, event | category | flops | bytes accessed | tf_op | source)
XLA Modules:
  0.0 39.4 jit_solution(5827761074020687503)
XLA Ops:
  0.0 0.0 copy-start.1
  0.0 0.0 copy-start.4
  0.0 0.0 copy-start.2
  0.0 0.0 copy-start.3
  0.0 0.0 copy-start
  0.0 2.8 %level_sum.1 = (bf16[2,80,256]{2,1,0:T(8,128)(2,1)S(1)}, bf16[2,80,256]{2,1,0:T(8,128)(2,1)S(1)}) custom-call(bf16[16,32,32,80]{3,2,1,0:T(8,128)(2,1)} %dev_hbm.1, f32[16,32,32]{2,1,0:T(8,128)} %misfit_hbm.1), custom_call_target="tpu_custom_call" | custom-call | tf_op jit(solution)/shard_map/level_sum/pallas_call | solution.py:208
  2.8 3.5 %collective-permute-start = (bf16[2,80,256]{2,1,0:T(8,128)(2,1)S(1)}, bf16[2,80,256]{2,1,0:T(8,128)(2,1)S(1)}, u32[]{:S(2)}, u32[]{:S(2)}) collective-permute-start(bf16[2,80,256]{2,1,0:T(8,128)(2,1)S(1)} %get-tuple-element.11.right_ref), channel_id=1, source_target_pairs={{0,1},{1,2},{2,3},{3,4},{4,5},{5,6},{6,7},{7,8},{8,9},{9,10},{10,1... | collective-permute-start | bytes 245768 | tf_op jit(solution)/shard_map/ppermute | solution.py:224
  6.4 16.8 %collective-permute-start.1 = (bf16[2,80,256]{2,1,0:T(8,128)(2,1)S(1)}, bf16[2,80,256]{2,1,0:T(8,128)(2,1)S(1)}, u32[]{:S(2)}, u32[]{:S(2)}) collective-permute-start(bf16[2,80,256]{2,1,0:T(8,128)(2,1)S(1)} %get-tuple-element.12.left_ref), channel_id=1, source_target_pairs={{0,31},{1,0},{2,1},{3,2},{4,3},{5,4},{6,5},{7,6},{8,7},{9,8},{10,9... | collective-permute-start | bytes 245768 | tf_op jit(solution)/shard_map/ppermute | solution.py:224
  23.1 0.2 collective-permute-done.low_ref
  23.3 1.3 %collective-permute-done.1.high_ref = bf16[2,80,256]{2,1,0:T(8,128)(2,1)S(1)} collective-permute-done((bf16[2,80,256]{2,1,0:T(8,128)(2,1)S(1)}, bf16[2,80,256]{2,1,0:T(8,128)(2,1)S(1)}, u32[]{:S(2)}, u32[]{:S(2)}) %collective-permute-start.1) | collective-permute-done | bytes 81952 | tf_op jit(solution)/shard_map/ppermute | solution.py:224
  24.6 3.2 %collective-permute-start.2 = (bf16[4,80,256]{2,1,0:T(8,128)(2,1)S(1)}, bf16[4,80,256]{2,1,0:T(8,128)(2,1)S(1)}, u32[]{:S(2)}, u32[]{:S(2)}) collective-permute-start(bf16[4,80,256]{2,1,0:T(8,128)(2,1)S(1)} %get-tuple-element.13), channel_id=1, source_target_pairs={{0,32},{32,64},{64,96},{96,128},{128,160},{160,192},{192,224},{224... | collective-permute-start | bytes 491528 | tf_op jit(solution)/shard_map/ppermute | solution.py:224
  27.8 2.2 %collective-permute-start.3 = (bf16[4,80,256]{2,1,0:T(8,128)(2,1)S(1)}, bf16[4,80,256]{2,1,0:T(8,128)(2,1)S(1)}, u32[]{:S(2)}, u32[]{:S(2)}) collective-permute-start(bf16[4,80,256]{2,1,0:T(8,128)(2,1)S(1)} %get-tuple-element.14), channel_id=1, source_target_pairs={{0,992},{32,0},{64,32},{96,64},{128,96},{160,128},{192,160},{224,1... | collective-permute-start | bytes 491528 | tf_op jit(solution)/shard_map/ppermute | solution.py:224
  30.7 0.0 copy-done.1
  30.7 0.0 copy-done.4
  30.7 0.0 copy-done.2
  30.7 0.0 copy-done.3
  30.7 0.0 copy-done
  30.7 1.0 %inner.1 = (f32[1,1024]{1,0:T(1,128)S(1)}, f32[1,1024]{1,0:T(1,128)S(1)}) custom-call(s32[1,1]{1,0:T(1,128)S(6)} %copy.9.tally_hbm, bf16[2,80,256]{2,1,0:T(8,128)(2,1)S(1)} %get-tuple-element.12.left_ref, bf16[2,80,256]{2,1,0:T(8,128)(2,1)S(1)} %get-tuple-element.11.right_ref, s32[2,1024]{1,0:T(2,128)S(1)} %bitcast.12, s32[1,1024]{1,0:T(1,128)S(1)} %bitcast.16, ...), custom_call_target="tpu_custom_call" | custom-call | flops 167772160 | bytes 327680 | tf_op jit(solution)/shard_map/inner/pallas_call | solution.py:238
  31.7 0.6 %sides.1.sides_ref = f32[1,1024]{1,0:T(1,128)S(1)} custom-call(bf16[2,80,256]{2,1,0:T(8,128)(2,1)S(1)} %collective-permute-done.low_ref, bf16[2,80,256]{2,1,0:T(8,128)(2,1)S(1)} %collective-permute-done.1.high_ref, s32[2,1024]{1,0:T(2,128)S(1)} %bitcast.13, s32[1,1024]{1,0:T(1,128)S(1)} %bitcast.17, s32[4,1024]{1,0:T(4,128)S(1)} %bitcast.10, ...), custom_call_target="tpu_custom_call" | custom-call | flops 167772160 | bytes 327680 | tf_op jit(solution)/shard_map/sides/pallas_call | solution.py:256
  32.3 0.0 collective-permute-done.2.above_ref
  32.3 5.4 %collective-permute-done.3.below_ref = bf16[4,80,256]{2,1,0:T(8,128)(2,1)S(1)} collective-permute-done((bf16[4,80,256]{2,1,0:T(8,128)(2,1)S(1)}, bf16[4,80,256]{2,1,0:T(8,128)(2,1)S(1)}, u32[]{:S(2)}, u32[]{:S(2)}) %collective-permute-start.3) | collective-permute-done | bytes 163872 | tf_op jit(solution)/shard_map/ppermute | solution.py:224
  37.8 1.6 %outer.1 = f32[1,1024]{1,0:T(1,128)} custom-call(bf16[4,80,256]{2,1,0:T(8,128)(2,1)S(1)} %collective-permute-done.2.above_ref, bf16[4,80,256]{2,1,0:T(8,128)(2,1)S(1)} %collective-permute-done.3.below_ref, s32[2,1024]{1,0:T(2,128)S(1)} %bitcast.14, s32[1,1024]{1,0:T(1,128)S(1)} %bitcast.18, s32[4,1024]{1,0:T(4,128)S(1)} %bitcast.11, ...), custom_call_target="tpu_custom_call" | custom-call | flops 335544320 | bytes 327680 | tf_op jit(solution)/shard_map/outer/pallas_call | solution.py:264
  (1 shorter events, 0.0 us)
Async XLA Ops:
  0.0 30.7 %copy-start.1 = (s32[1,1,4,1024]{3,2,1,0:T(4,128)S(1)}, s32[1,1,4,1024]{3,2,1,0:T(4,128)}, u32[]{:S(2)}) copy-start(s32[1,1,4,1024]{3,2,1,0:T(4,128)} %param.14) | copy-start | bytes 49156
  0.0 30.7 %copy-start.4 = (s32[1,1,1024]{2,1,0:T(1,128)S(1)}, s32[1,1,1024]{2,1,0:T(1,128)}, u32[]{:S(2)}) copy-start(s32[1,1,1024]{2,1,0:T(1,128)} %param.13) | copy-start | bytes 12292
  0.0 30.7 %copy-start.2 = (s32[1,1,2,1024]{3,2,1,0:T(2,128)S(1)}, s32[1,1,2,1024]{3,2,1,0:T(2,128)}, u32[]{:S(2)}) copy-start(s32[1,1,2,1024]{3,2,1,0:T(2,128)} %param.12) | copy-start | bytes 24580
  0.0 30.7 %copy-start.3 = (f32[1,1,1024]{2,1,0:T(1,128)S(1)}, f32[1,1,1024]{2,1,0:T(1,128)}, u32[]{:S(2)}) copy-start(f32[1,1,1024]{2,1,0:T(1,128)} %param.11) | copy-start | bytes 12292
  0.0 30.7 %copy-start = (bf16[1,1,80,1024]{3,2,1,0:T(8,128)(2,1)S(1)}, bf16[1,1,80,1024]{3,2,1,0:T(8,128)(2,1)}, u32[]{:S(2)}) copy-start(bf16[1,1,80,1024]{3,2,1,0:T(8,128)(2,1)} %param.10) | copy-start | bytes 491524
  2.8 20.5 %collective-permute-start = (bf16[2,80,256]{2,1,0:T(8,128)(2,1)S(1)}, bf16[2,80,256]{2,1,0:T(8,128)(2,1)S(1)}, u32[]{:S(2)}, u32[]{:S(2)}) collective-permute-start(bf16[2,80,256]{2,1,0:T(8,128)(2,1)S(1)} %get-tuple-element.11.right_ref), channel_id=1, source_target_pairs={{0,1},{1,2},{2,3},{3,4},{4,5},{5,6},{6,7},{7,8},{8,9},{9,10},{10,1... | collective-permute-start | bytes 245768 | tf_op jit(solution)/shard_map/ppermute | solution.py:224
  6.4 18.2 %collective-permute-start.1 = (bf16[2,80,256]{2,1,0:T(8,128)(2,1)S(1)}, bf16[2,80,256]{2,1,0:T(8,128)(2,1)S(1)}, u32[]{:S(2)}, u32[]{:S(2)}) collective-permute-start(bf16[2,80,256]{2,1,0:T(8,128)(2,1)S(1)} %get-tuple-element.12.left_ref), channel_id=1, source_target_pairs={{0,31},{1,0},{2,1},{3,2},{4,3},{5,4},{6,5},{7,6},{8,7},{9,8},{10,9... | collective-permute-start | bytes 245768 | tf_op jit(solution)/shard_map/ppermute | solution.py:224
  24.6 7.7 %collective-permute-start.2 = (bf16[4,80,256]{2,1,0:T(8,128)(2,1)S(1)}, bf16[4,80,256]{2,1,0:T(8,128)(2,1)S(1)}, u32[]{:S(2)}, u32[]{:S(2)}) collective-permute-start(bf16[4,80,256]{2,1,0:T(8,128)(2,1)S(1)} %get-tuple-element.13), channel_id=1, source_target_pairs={{0,32},{32,64},{64,96},{96,128},{128,160},{160,192},{192,224},{224... | collective-permute-start | bytes 491528 | tf_op jit(solution)/shard_map/ppermute | solution.py:224
  27.8 10.0 %collective-permute-start.3 = (bf16[4,80,256]{2,1,0:T(8,128)(2,1)S(1)}, bf16[4,80,256]{2,1,0:T(8,128)(2,1)S(1)}, u32[]{:S(2)}, u32[]{:S(2)}) collective-permute-start(bf16[4,80,256]{2,1,0:T(8,128)(2,1)S(1)} %get-tuple-element.14), channel_id=1, source_target_pairs={{0,992},{32,0},{64,32},{96,64},{128,96},{160,128},{192,160},{224,1... | collective-permute-start | bytes 491528 | tf_op jit(solution)/shard_map/ppermute | solution.py:224

commit v2 on v1

--- a/solution.py
+++ b/solution.py
@@ -1,3 +1,5 @@
+import functools
+
 import jax
 import jax.numpy as jnp
 from jax import lax
@@ -53,71 +55,75 @@
             outs[h][c // per, :, (c % per) * width : (c % per + 1) * width] = group
 
 
-def assemble_kernel(low_ref, left_ref, right_ref, high_ref, top_ref, bottom_ref):
+def assemble_kernel(low_ref, left_ref, right_ref, high_ref, after_ref, across_ref, within_ref):
+    odd = lax.axis_index("lat") % 2
     for i, ref in enumerate((low_ref, left_ref, right_ref, high_ref)):
-        top_ref[i] = ref[0]
-        bottom_ref[i] = ref[1]
+        across_ref[i] = ref[odd]
+        within_ref[i] = ref[1 - odd]
 
 
 def tables(place_ref, class_ref, codes_ref, col_bands, row_bands):
     shape = (HALF, place_ref.shape[1])
-    u = jnp.broadcast_to(place_ref[0:1, :], shape).astype(F32).astype(BF16)
-    v = place_ref[1:2, :]
     x = lax.broadcasted_iota(jnp.int32, shape, 0)
     side = HALF // 4 * (1 + class_ref[...])
     radius_sq = side * side
     column = {}
     for band in col_bands:
-        gap = x + HALF * (band - 1) - v
+        gap = x + HALF * (band - 1) - place_ref[1:2, :]
         column[band] = (gap * gap).astype(F32).astype(BF16)
-    reach = {}
-    for band_row in row_bands:
+    rows, reach = [], []
+    for first, dr in row_bands:
+        rows.append(jnp.broadcast_to(place_ref[0:1, :] - first, shape).astype(F32).astype(BF16))
+        limits = {}
         for band in col_bands:
-            dr, ds = (band_row + 1) // 2, (band + 1) // 2
-            if (dr, ds) in reach:
+            ds = (band + 1) // 2
+            if ds in limits:
                 continue
             code = 3 * dr + ds
             named = codes_ref[0:1, :] == code
             for e in range(1, 4):
                 named = named | (codes_ref[e : e + 1, :] == code)
             kept = jnp.where(named, radius_sq, 0)
-            reach[dr, ds] = jnp.broadcast_to(kept, shape).astype(F32).astype(BF16)
-    return u, column, reach
-
-
-def project(window, place_ref, class_ref, codes_ref, blocks):
-    col_bands = sorted({b for _, b, _ in blocks})
-    row_bands = sorted({a for a, _, _ in blocks})
-    u, column, reach = tables(place_ref, class_ref, codes_ref, col_bands, row_bands)
+            limits[ds] = jnp.broadcast_to(kept, shape).astype(F32).astype(BF16)
+        reach.append(limits)
+    return rows, column, reach
+
+
+def project(place_ref, class_ref, codes_ref, row_bands, col_bands, window):
+    rows, column, reach = tables(place_ref, class_ref, codes_ref, col_bands, row_bands)
     slots = place_ref.shape[1]
     wide = 256
     parts = []
     for n in range(slots // wide):
         cut = slice(n * wide, (n + 1) * wide)
         total = None
-        for row_band in row_bands:
+        for i in range(len(row_bands)):
             squares = []
             for y in range(HALF):
-                gap = jnp.asarray(y + HALF * (row_band - 1), BF16) - u[:, cut]
+                gap = jnp.asarray(y, BF16) - rows[i][:, cut]
                 squares.append(gap * gap)
-            for a, b, source in blocks:
-                if a != row_band:
-                    continue
-                limit = reach[(a + 1) // 2, (b + 1) // 2][:, cut]
-                across = column[b][:, cut]
+            for j, band in enumerate(col_bands):
+                limit = reach[i][(band + 1) // 2][:, cut]
+                across = column[band][:, cut]
                 pieces = []
                 for y in range(HALF):
                     m = jnp.maximum((limit - squares[y]) - across, jnp.asarray(0, BF16))
                     pieces.append(m * m)
                 taper = jnp.concatenate(pieces, axis=0)
-                term = jnp.dot(window(source), taper, preferred_element_type=F32)
+                term = jnp.dot(window(i, j), taper, preferred_element_type=F32)
                 total = term if total is None else total + term
         parts.append(total)
     return parts
 
 
-def reduce_kernel(window, blocks, place_ref, class_ref, codes_ref, sensed_ref, out_ref):
-    parts = project(window, place_ref, class_ref, codes_ref, blocks)
+OWN_ROWS = ((0, 1), (HALF, 1))
+
+
+def reduce_kernel(first_ref, second_ref, place_ref, class_ref, codes_ref, sensed_ref, out_ref, cols):
+    refs = (first_ref, second_ref)
+    parts = project(
+        place_ref, class_ref, codes_ref, OWN_ROWS, cols, lambda row, col: refs[col][row]
+    )
     for n, part in enumerate(parts):
         wide = part.shape[1]
         cut = slice(n * wide, (n + 1) * wide)
@@ -125,7 +131,7 @@
 
 
 def inner_kernel(
-    tally_hbm,
+    tally_ref,
     left_ref,
     right_ref,
     place_ref,
@@ -135,53 +141,39 @@
     scaled_ref,
     out_ref,
     weight_ref,
-    tally_ref,
-    sem,
 ):
-    copy = pltpu.make_async_copy(tally_hbm, tally_ref, sem)
-    copy.start()
-    blocks = [(1 + y, 1 + h, (h, y)) for h in range(2) for y in range(2)]
-    refs = (left_ref, right_ref)
     reduce_kernel(
-        lambda s: refs[s[0]][s[1]], blocks, place_ref, class_ref, codes_ref, sensed_ref, out_ref
+        left_ref, right_ref, place_ref, class_ref, codes_ref, sensed_ref, out_ref, (1, 2)
     )
     side = (HALF // 4 * (1 + class_ref[...])).astype(F32)
     radius_sq = side * side
     weight = scaled_ref[...] / (radius_sq * radius_sq) / (sensed_ref.shape[0] - 1)
     slot = lax.broadcasted_iota(jnp.int32, weight.shape, 1)
-    copy.wait()
     weight_ref[...] = jnp.where(slot < tally_ref[0, 0], weight, 0.0)
 
 
 def sides_kernel(low_ref, high_ref, place_ref, class_ref, codes_ref, sensed_ref, out_ref):
-    blocks = [(1 + y, 3 * h, (h, y)) for h in range(2) for y in range(2)]
-    refs = (low_ref, high_ref)
-    reduce_kernel(
-        lambda s: refs[s[0]][s[1]], blocks, place_ref, class_ref, codes_ref, sensed_ref, out_ref
-    )
-
-
-def outer_kernel(
-    above_ref,
-    below_ref,
-    place_ref,
-    class_ref,
-    codes_ref,
-    sensed_ref,
-    inner_ref,
-    sides_ref,
-    weight_ref,
-    out_ref,
-):
-    blocks = [(3 * h, b, (h, b)) for h in range(2) for b in range(4)]
-    refs = (above_ref, below_ref)
-    parts = project(lambda s: refs[s[0]][s[1]], place_ref, class_ref, codes_ref, blocks)
+    reduce_kernel(low_ref, high_ref, place_ref, class_ref, codes_ref, sensed_ref, out_ref, (0, 3))
+
+
+def strip_kernel(across, strip_ref, place_ref, class_ref, codes_ref, sensed_ref, *refs):
+    odd = lax.axis_index("lat") % 2
+    below = odd if across else 1 - odd
+    row_bands = ((3 * HALF * below - HALF, 2 * below),)
+    parts = project(
+        place_ref, class_ref, codes_ref, row_bands, (0, 1, 2, 3), lambda row, col: strip_ref[col]
+    )
+    *others, out_ref = refs
     for n, part in enumerate(parts):
         wide = part.shape[1]
         cut = slice(n * wide, (n + 1) * wide)
         summed = jnp.sum(part * sensed_ref[:, cut].astype(F32), axis=0, keepdims=True)
-        summed = summed + inner_ref[:, cut] + sides_ref[:, cut]
-        out_ref[:, cut] = weight_ref[:, cut] * summed
+        if others:
+            weight_ref, *sums = others
+            for ref in sums:
+                summed = summed + ref[:, cut]
+            summed = weight_ref[:, cut] * summed
+        out_ref[:, cut] = summed
 
 
 def on_device(
@@ -238,21 +230,28 @@
     inner, weight = pl.pallas_call(
         inner_kernel,
         out_shape=(line, line),
-        in_specs=[anywhere] + [vmem] * 7,
+        in_specs=[pl.BlockSpec(memory_space=pltpu.SMEM)] + [vmem] * 7,
         out_specs=(vmem, vmem),
-        scratch_shapes=[pltpu.SMEM((1, 1), jnp.int32), pltpu.SemaphoreType.DMA],
         cost_estimate=cost(4),
         name="inner",
     )(active_datum_tally, *near(left, right, place, category, codes, sensed, scaled_departure[0]))
-    top, bottom = pl.pallas_call(
+    across, within = pl.pallas_call(
         assemble_kernel,
         out_shape=(strip, strip),
-        in_specs=[vmem] * 4,
+        in_specs=[vmem] * 5,
         out_specs=(vmem, vmem),
         name="assemble",
-    )(*near(low, left, right, high))
-    above = shift(bottom, "lat", 1)
-    below = shift(top, "lat", -1)
+    )(*near(low, left, right, high, inner))
+
+    def swap(block, first):
+        count = lax.axis_size("lat")
+        lower = range(first, count - 1, 2)
+        return lax.ppermute(
+            block, "lat", [(i, i + 1) for i in lower] + [(i + 1, i) for i in lower]
+        )
+
+    across = swap(across, 1)
+    within = swap(within, 0)
     sides = pl.pallas_call(
         sides_kernel,
         out_shape=line,
@@ -261,14 +260,22 @@
         cost_estimate=cost(4),
         name="sides",
     )(*near(low, high, place, category, codes, sensed))
+    within = pl.pallas_call(
+        functools.partial(strip_kernel, False),
+        out_shape=line,
+        in_specs=[vmem] * 5,
+        out_specs=vmem,
+        cost_estimate=cost(4),
+        name="within_strip",
+    )(*near(within, place, category, codes, sensed))
     impact = pl.pallas_call(
-        outer_kernel,
+        functools.partial(strip_kernel, True),
         out_shape=jax.ShapeDtypeStruct((1, slots), F32),
         in_specs=[vmem] * 9,
         out_specs=vmem,
-        cost_estimate=cost(8),
-        name="outer",
-    )(*near(above, below, place, category, codes, sensed, inner, sides, weight))
+        cost_estimate=cost(4),
+        name="across_strip",
+    )(*near(across, place, category, codes, sensed, weight, inner, sides, within))
     return impact[None]
 
 

time: 39.6 us -> 38.3 us (0.967)
  the two profiles are of different devices: /device:TPU:31 before, /device:TPU:29 now
where the time goes in v2:
time: 38.3 us; the launch traced here: 38 us
  starting transfers between devices  26.1 us (68%)
  Pallas kernels  5.8 us (15%)
  waiting for transfers between devices  5.29 us (14%)
  between operations  0.79 us (2%)
    ppermute x2, starting transfers between devices, shift(): lax.ppermute(block, axis, [(i, (i + by) % count) for i in range(count)])  20.3 us
    ppermute x2, starting transfers between devices, swap(): lax.ppermute(block, 'lat', [(i, i + 1) for i in lower] + [(i + 1, i) for...  5.82 us
    ppermute x2, waiting for transfers between devices, swap(): lax.ppermute(block, 'lat', [(i, i + 1) for i in lower] + [(i + 1, i) for...  5.11 us
    pallas_call x1, Pallas kernels, on_device(): pl.pallas_call(level_sum_kernel, out_shape=(half, half), in_specs=[anywhe...  2.77 us
    pallas_call x1, Pallas kernels, on_device(): pl.pallas_call(functools.partial(strip_kernel, True), out_shape=jax.Shape...  1.2 us
  transfers between devices with their start and end apart: 4, of which 2 were waited for; matrix products, arithmetic and copies ran while one was open for 0% of the time, Pallas kernels for 5%

profile of v2, /device:TPU:29, one launch (start us, length us, event | category | flops | bytes accessed | tf_op | source)
XLA Modules:
  0.0 38.0 jit_solution(9943573872764068855)
XLA Ops:
  0.0 0.0 copy-start.1
  0.0 0.0 copy-start.4
  0.0 0.0 copy-start.2
  0.0 0.0 copy-start.3
  0.0 0.0 copy-start
  0.0 2.8 %level_sum.1 = (bf16[2,80,256]{2,1,0:T(8,128)(2,1)S(1)}, bf16[2,80,256]{2,1,0:T(8,128)(2,1)S(1)}) custom-call(bf16[16,32,32,80]{3,2,1,0:T(8,128)(2,1)} %dev_hbm.1, f32[16,32,32]{2,1,0:T(8,128)} %misfit_hbm.1), custom_call_target="tpu_custom_call" | custom-call | tf_op jit(solution)/shard_map/level_sum/pallas_call | solution.py:200
  2.8 3.5 %collective-permute-start = (bf16[2,80,256]{2,1,0:T(8,128)(2,1)S(1)}, bf16[2,80,256]{2,1,0:T(8,128)(2,1)S(1)}, u32[]{:S(2)}, u32[]{:S(2)}) collective-permute-start(bf16[2,80,256]{2,1,0:T(8,128)(2,1)S(1)} %get-tuple-element.11.right_ref), channel_id=1, source_target_pairs={{0,1},{1,2},{2,3},{3,4},{4,5},{5,6},{6,7},{7,8},{8,9},{9,10},{10,1... | collective-permute-start | bytes 245768 | tf_op jit(solution)/shard_map/ppermute | solution.py:216
  6.4 16.8 %collective-permute-start.1 = (bf16[2,80,256]{2,1,0:T(8,128)(2,1)S(1)}, bf16[2,80,256]{2,1,0:T(8,128)(2,1)S(1)}, u32[]{:S(2)}, u32[]{:S(2)}) collective-permute-start(bf16[2,80,256]{2,1,0:T(8,128)(2,1)S(1)} %get-tuple-element.12.left_ref), channel_id=1, source_target_pairs={{0,31},{1,0},{2,1},{3,2},{4,3},{5,4},{6,5},{7,6},{8,7},{9,8},{10,9... | collective-permute-start | bytes 245768 | tf_op jit(solution)/shard_map/ppermute | solution.py:216
  23.8 0.0 copy-done.1
  23.8 0.0 copy-done.4
  23.8 0.0 copy-done.2
  23.8 0.0 copy-done.3
  23.8 0.0 copy-done
  23.8 0.6 %inner.1 = (f32[1,1024]{1,0:T(1,128)S(1)}, f32[1,1024]{1,0:T(1,128)S(1)}) custom-call(s32[1,1]{1,0:T(1,128)S(6)} %copy.9.tally_ref, bf16[2,80,256]{2,1,0:T(8,128)(2,1)S(1)} %get-tuple-element.12.left_ref, bf16[2,80,256]{2,1,0:T(8,128)(2,1)S(1)} %get-tuple-element.11.right_ref, s32[2,1024]{1,0:T(2,128)S(1)} %bitcast.14, s32[1,1024]{1,0:T(1,128)S(1)} %bitcast.19, ...), custom_call_target="tpu_custom_call" | custom-call | flops 167772160 | bytes 327680 | tf_op jit(solution)/shard_map/inner/pallas_call | solution.py:230
  24.4 0.0 collective-permute-done.low_ref
  24.4 0.2 collective-permute-done.1.high_ref
  24.6 3.4 %collective-permute-start.3 = (bf16[4,80,256]{2,1,0:T(8,128)(2,1)S(1)}, bf16[4,80,256]{2,1,0:T(8,128)(2,1)S(1)}, u32[]{:S(2)}, u32[]{:S(2)}) collective-permute-start(bf16[4,80,256]{2,1,0:T(8,128)(2,1)S(1)} %get-tuple-element.16), channel_id=1, source_target_pairs={{0,32},{64,96},{128,160},{192,224},{256,288},{320,352},{384,416},{... | collective-permute-start | bytes 491528 | tf_op jit(solution)/shard_map/ppermute | solution.py:249
  28.1 2.4 %collective-permute-start.2 = (bf16[4,80,256]{2,1,0:T(8,128)(2,1)S(1)}, bf16[4,80,256]{2,1,0:T(8,128)(2,1)S(1)}, u32[]{:S(2)}, u32[]{:S(2)}) collective-permute-start(bf16[4,80,256]{2,1,0:T(8,128)(2,1)S(1)} %get-tuple-element.14), channel_id=1, source_target_pairs={{32,64},{96,128},{160,192},{224,256},{288,320},{352,384},{416,448}... | collective-permute-start | bytes 491528 | tf_op jit(solution)/shard_map/ppermute | solution.py:249
  30.5 0.6 %sides.1.refs_2_ = f32[1,1024]{1,0:T(1,128)S(1)} custom-call(bf16[2,80,256]{2,1,0:T(8,128)(2,1)S(1)} %collective-permute-done.low_ref, bf16[2,80,256]{2,1,0:T(8,128)(2,1)S(1)} %collective-permute-done.1.high_ref, s32[2,1024]{1,0:T(2,128)S(1)} %bitcast.15, s32[1,1024]{1,0:T(1,128)S(1)} %bitcast.20, s32[4,1024]{1,0:T(4,128)S(1)} %bitcast.11, ...), custom_call_target="tpu_custom_call" | custom-call | flops 167772160 | bytes 327680 | tf_op jit(solution)/shard_map/sides/pallas_call | solution.py:255
  31.1 0.0 collective-permute-done.3.strip_ref
  31.1 0.6 %within_strip.1.refs_3_ = f32[1,1024]{1,0:T(1,128)S(1)} custom-call(bf16[4,80,256]{2,1,0:T(8,128)(2,1)S(1)} %collective-permute-done.3.strip_ref, s32[2,1024]{1,0:T(2,128)S(1)} %bitcast.16, s32[1,1024]{1,0:T(1,128)S(1)} %bitcast.21, s32[4,1024]{1,0:T(4,128)S(1)} %bitcast.12, bf16[80,1024]{1,0:T(8,128)(2,1)S(1)} %bitcast.8), custom_call_target="tpu_custom_call" | custom-call | flops 167772160 | bytes 327680 | tf_op jit(solution)/shard_map/within_strip/pallas_call | solution.py:263
  31.7 5.1 %collective-permute-done.2.strip_ref = bf16[4,80,256]{2,1,0:T(8,128)(2,1)S(1)} collective-permute-done((bf16[4,80,256]{2,1,0:T(8,128)(2,1)S(1)}, bf16[4,80,256]{2,1,0:T(8,128)(2,1)S(1)}, u32[]{:S(2)}, u32[]{:S(2)}) %collective-permute-start.2) | collective-permute-done | bytes 163872 | tf_op jit(solution)/shard_map/ppermute | solution.py:249
  36.8 1.2 %across_strip.1 = f32[1,1024]{1,0:T(1,128)} custom-call(bf16[4,80,256]{2,1,0:T(8,128)(2,1)S(1)} %collective-permute-done.2.strip_ref, s32[2,1024]{1,0:T(2,128)S(1)} %bitcast.17, s32[1,1024]{1,0:T(1,128)S(1)} %bitcast.22, s32[4,1024]{1,0:T(4,128)S(1)} %bitcast.13, bf16[80,1024]{1,0:T(8,128)(2,1)S(1)} %bitcast.9, f32[1,1024]{1,0:T(1,128)S(1)} %get-tuple-element.15.refs_0_, ...), custom_call_target="tpu_custom_call" | custom-call | flops 167772160 | bytes 327680 | tf_op jit(solution)/shard_map/across_strip/pallas_call | solution.py:271
  (1 shorter events, 0.0 us)
Async XLA Ops:
  0.0 23.8 %copy-start.1 = (s32[1,1,4,1024]{3,2,1,0:T(4,128)S(1)}, s32[1,1,4,1024]{3,2,1,0:T(4,128)}, u32[]{:S(2)}) copy-start(s32[1,1,4,1024]{3,2,1,0:T(4,128)} %param.14) | copy-start | bytes 49156
  0.0 23.8 %copy-start.4 = (s32[1,1,1024]{2,1,0:T(1,128)S(1)}, s32[1,1,1024]{2,1,0:T(1,128)}, u32[]{:S(2)}) copy-start(s32[1,1,1024]{2,1,0:T(1,128)} %param.13) | copy-start | bytes 12292
  0.0 23.8 %copy-start.2 = (s32[1,1,2,1024]{3,2,1,0:T(2,128)S(1)}, s32[1,1,2,1024]{3,2,1,0:T(2,128)}, u32[]{:S(2)}) copy-start(s32[1,1,2,1024]{3,2,1,0:T(2,128)} %param.12) | copy-start | bytes 24580
  0.0 23.8 %copy-start.3 = (f32[1,1,1024]{2,1,0:T(1,128)S(1)}, f32[1,1,1024]{2,1,0:T(1,128)}, u32[]{:S(2)}) copy-start(f32[1,1,1024]{2,1,0:T(1,128)} %param.11) | copy-start | bytes 12292
  0.0 23.8 %copy-start = (bf16[1,1,80,1024]{3,2,1,0:T(8,128)(2,1)S(1)}, bf16[1,1,80,1024]{3,2,1,0:T(8,128)(2,1)}, u32[]{:S(2)}) copy-start(bf16[1,1,80,1024]{3,2,1,0:T(8,128)(2,1)} %param.10) | copy-start | bytes 491524
  2.8 21.6 %collective-permute-start = (bf16[2,80,256]{2,1,0:T(8,128)(2,1)S(1)}, bf16[2,80,256]{2,1,0:T(8,128)(2,1)S(1)}, u32[]{:S(2)}, u32[]{:S(2)}) collective-permute-start(bf16[2,80,256]{2,1,0:T(8,128)(2,1)S(1)} %get-tuple-element.11.right_ref), channel_id=1, source_target_pairs={{0,1},{1,2},{2,3},{3,4},{4,5},{5,6},{6,7},{7,8},{8,9},{9,10},{10,1... | collective-permute-start | bytes 245768 | tf_op jit(solution)/shard_map/ppermute | solution.py:216
  6.4 18.2 %collective-permute-start.1 = (bf16[2,80,256]{2,1,0:T(8,128)(2,1)S(1)}, bf16[2,80,256]{2,1,0:T(8,128)(2,1)S(1)}, u32[]{:S(2)}, u32[]{:S(2)}) collective-permute-start(bf16[2,80,256]{2,1,0:T(8,128)(2,1)S(1)} %get-tuple-element.12.left_ref), channel_id=1, source_target_pairs={{0,31},{1,0},{2,1},{3,2},{4,3},{5,4},{6,5},{7,6},{8,7},{9,8},{10,9... | collective-permute-start | bytes 245768 | tf_op jit(solution)/shard_map/ppermute | solution.py:216
  24.6 6.5 %collective-permute-start.3 = (bf16[4,80,256]{2,1,0:T(8,128)(2,1)S(1)}, bf16[4,80,256]{2,1,0:T(8,128)(2,1)S(1)}, u32[]{:S(2)}, u32[]{:S(2)}) collective-permute-start(bf16[4,80,256]{2,1,0:T(8,128)(2,1)S(1)} %get-tuple-element.16), channel_id=1, source_target_pairs={{0,32},{64,96},{128,160},{192,224},{256,288},{320,352},{384,416},{... | collective-permute-start | bytes 491528 | tf_op jit(solution)/shard_map/ppermute | solution.py:249
  28.1 8.7 %collective-permute-start.2 = (bf16[4,80,256]{2,1,0:T(8,128)(2,1)S(1)}, bf16[4,80,256]{2,1,0:T(8,128)(2,1)S(1)}, u32[]{:S(2)}, u32[]{:S(2)}) collective-permute-start(bf16[4,80,256]{2,1,0:T(8,128)(2,1)S(1)} %get-tuple-element.14), channel_id=1, source_target_pairs={{32,64},{96,128},{160,192},{224,256},{288,320},{352,384},{416,448}... | collective-permute-start | bytes 491528 | tf_op jit(solution)/shard_map/ppermute | solution.py:249
